TPU v7x, 32 devices: a whole 2x2x4 slice. The times are simulated.
32 devices in a mesh: dp: 2 (over x), ep: 16 (over z, y, core).
Axes of the slice: x: 2, y: 2, z: 4, core: 2. Of those that a mesh axis runs over, the one named last changes fastest.
Arguments:
- tokens: bfloat16 [256, 3584], P(('dp', 'ep')), may hold values from -6 to 6
- expert_ids: int32 [2, 256, 8], P(None, ('dp', 'ep')), may hold values from 0 to 15, all different within a row; in each aligned block of 8 rows (0 to 7, 8 to 15, ..., all dimensions but the last counted through in order) at most 6 rows name the same one
- quant_gates: int32 [2, 256, 8], P(None, ('dp', 'ep')), may hold values from 1 to 63
- w_gate: bfloat16 [2, 16, 3584, 1024], P(None, 'ep', None, 'dp'), may hold values from -0.09375 to 0.09375
- w_up: bfloat16 [2, 16, 3584, 1024], P(None, 'ep', None, 'dp'), may hold values from -0.09375 to 0.09375
- w_down: bfloat16 [2, 16, 1024, 3584], P(None, 'ep', 'dp'), may hold values from -0.1875 to 0.1875
Outputs:
- stream_out: bfloat16 [256, 3584], P(('dp', 'ep'))
- expert_load: int32 [2, 16], replicated
Inputs may be any that keep to these rules, and one draw needn't show every extreme that they name: `expert_ids`: in each layer, the 8 tokens of one device name any one expert at most 6 times, a bound that some block reaches.
All inputs are finite; a program needn't handle non-finite values.
Results may differ from a plain program's by a relative error of at most 0.015.
Values may be sent and summed in bfloat16 or wider, within the bound.
A program may use at most 64 MiB of HBM per device.

v0:
```python
import jax
import jax.numpy as jnp
from jax import lax
from jax.sharding import PartitionSpec as P

ROUTE_SCALE = 2.827
EPS = 1e-06


def slot_tables(ids, quant, experts, capacity):
    count_tok, top = ids.shape
    flat = ids.reshape(count_tok * top)
    expert_iota = lax.broadcasted_iota(jnp.int32, (count_tok * top, experts), 1)
    onehot = (flat[:, None] == expert_iota).astype(jnp.int32)
    earlier = jnp.cumsum(onehot, axis=0) - onehot
    position = jnp.sum(earlier * onehot, axis=1)
    target = flat * capacity + position
    slot_iota = lax.broadcasted_iota(jnp.int32, (count_tok * top, experts * capacity), 1)
    picked = target[:, None] == slot_iota
    quant_wide = quant.astype(jnp.float32)
    gates = (ROUTE_SCALE * quant_wide / jnp.sum(quant_wide, axis=1, keepdims=True)).reshape(
        count_tok * top
    )
    spread = jnp.sum(
        jnp.where(picked, gates[:, None], 0.0).reshape(count_tok, top, experts * capacity), axis=1
    )
    chosen = jnp.sum(picked.astype(jnp.float32).reshape(count_tok, top, experts * capacity), axis=1)
    counts = jnp.sum(onehot, axis=0)
    return (chosen, spread, counts)


def per_device(tokens, expert_ids, quant_gates, w_gate, w_up, w_down):
    layers, count_tok, top = expert_ids.shape
    n_ep = lax.axis_size("ep")
    capacity = min(count_tok, max(2, 3 * count_tok * top // (2 * n_ep)))
    width = tokens.shape[1]
    state = tokens
    table = jnp.stack(
        [
            slot_tables(expert_ids[layer], quant_gates[layer], n_ep, capacity)[2]
            for layer in range(layers)
        ]
    )
    loads = lax.psum(table, ("dp", "ep"))
    for layer in range(layers):
        chosen, spread, counts = slot_tables(expert_ids[layer], quant_gates[layer], n_ep, capacity)
        wide = state.astype(jnp.float32)
        normed = (wide * lax.rsqrt(jnp.mean(wide * wide, axis=1, keepdims=True) + EPS)).astype(
            jnp.bfloat16
        )
        outgoing = jnp.dot(
            chosen.T.astype(jnp.bfloat16), normed, preferred_element_type=jnp.float32
        ).astype(jnp.bfloat16)
        arrived = lax.all_to_all(
            outgoing.reshape(n_ep, capacity, width), "ep", split_axis=0, concat_axis=0, tiled=True
        )
        arrived = arrived.reshape(n_ep * capacity, width)
        weight_gate = w_gate[layer, 0]
        weight_up = w_up[layer, 0]
        weight_down = w_down[layer, 0]
        piece = lax.all_gather(arrived, "dp", axis=0, tiled=True)
        gate = jnp.dot(piece, weight_gate, preferred_element_type=jnp.float32)
        upper = jnp.dot(piece, weight_up, preferred_element_type=jnp.float32)
        hidden = (jax.nn.silu(gate) * upper).astype(jnp.bfloat16)
        partial_out = jnp.dot(hidden, weight_down, preferred_element_type=jnp.float32)
        parts = partial_out.astype(jnp.bfloat16)
        summed = lax.psum_scatter(
            parts.astype(jnp.float32).astype(jnp.bfloat16), "dp", scatter_dimension=0, tiled=True
        ).astype(jnp.float32)
        returned = lax.all_to_all(
            summed.reshape(n_ep, capacity, width).astype(jnp.bfloat16),
            "ep",
            split_axis=0,
            concat_axis=0,
            tiled=True,
        ).astype(jnp.float32)
        branch = jnp.dot(
            spread,
            returned.reshape(n_ep * capacity, width),
            precision=lax.Precision.HIGHEST,
            preferred_element_type=jnp.float32,
        )
        state = (state.astype(jnp.float32) + branch).astype(jnp.bfloat16)
    return (state, loads)


def solution(mesh):
    return jax.shard_map(
        per_device,
        mesh=mesh,
        in_specs=(
            P(("dp", "ep"), None),
            P(None, ("dp", "ep"), None),
            P(None, ("dp", "ep"), None),
            P(None, "ep", None, "dp"),
            P(None, "ep", None, "dp"),
            P(None, "ep", "dp", None),
        ),
        out_specs=(P(("dp", "ep"), None), P()),
        check_vma=False,
    )
```

profile of v0, /device:TPU:0, one launch (start us, length us, event | category | flops | bytes accessed | tf_op | source)
XLA Modules:
  0.0 278.6 jit_solution(12670127936095068034)
XLA Ops:
  7.2 1.0 fusion.47
  8.2 0.9 convert_reduce_fusion.2
  9.0 0.7 fusion.60
  10.1 0.2 fusion.54
  10.8 0.8 bitcast_divide_fusion
  11.6 0.7 bitcast_add_fusion
  12.4 1.2 convolution_convert_fusion.3
  13.6 0.2 reshape.136
  13.9 29.6 %all_to_all.20 = bf16[16,6,3584]{2,1,0:T(8,128)(2,1)S(1)} all-to-all(bf16[16,6,3584]{2,1,0:T(8,128)(2,1)S(1)} %reshape.136), channel_id=1, replica_groups=mesh['dp'=2,'ep'=16] {'ep'}, dimensions={0} | all-to-all | bytes 1376256 | tf_op jit(solution)/shard_map/all_to_all | solution.py:54
  43.5 1.1 reshape.137
  44.7 24.9 %all-gather.3.cloned.1.call-done = bf16[192,3584]{1,0:T(8,128)(2,1)} async-done(((bf16[96,3584]{1,0:T(8,128)(2,1)}), bf16[192,3584]{1,0:T(8,128)(2,1)}) %all-gather.3.cloned.1.call-update) | async-done | bytes 1376272 | tf_op jit(solution)/shard_map/all_gather | solution.py:61
  69.6 3.4 %fusion.11 = f32[192,512]{1,0:T(8,128)S(1)} fusion(bf16[192,3584]{1,0:T(8,128)(2,1)} %all-gather.3.cloned.1.call-done, bf16[2,1,3584,512]{3,2,1,0:T(8,128)(2,1)} %param.9), kind=kOutput, calls=%fused_computation.17 | convolution fusion | flops 704643072 | bytes 5439488 | tf_op jit(solution)/shard_map/dot_general | solution.py:62
  73.0 5.9 %convolution_convert_fusion.1 = bf16[192,3584]{1,0:T(8,128)(2,1)} fusion(bf16[2,1,512,3584]{3,2,1,0:T(8,128)(2,1)} %param.11, bf16[192,3584]{1,0:T(8,128)(2,1)S(1)} %copy-done.1, bf16[2,1,3584,512]{3,2,1,0:T(8,128)(2,1)} %param.10, f32[192,512]{1,0:T(8,128)S(1)} %fusion.11), kind=kOutput, calls=%fused_computation.1 | convolution fusion | flops 1410564096 | bytes 10485760 | tf_op jit(solution)/shard_map/dot_general | solution.py:65
  79.0 24.1 %reduce-scatter.3.cloned.1.call-done = bf16[96,3584]{1,0:T(8,128)(2,1)} async-done(((bf16[192,3584]{1,0:T(8,128)(2,1)}), bf16[96,3584]{1,0:T(8,128)(2,1)}) %reduce-scatter.3.cloned.1.call-update) | async-done | bytes 688144 | tf_op jit(solution)/shard_map/reduce_scatter | solution.py:67
  103.2 2.1 convert_element_type.103
  105.3 5.6 %all-to-all-start.1 = ((bf16[16,6,3584]{2,1,0:T(8,128)(2,1)}), bf16[16,6,3584]{2,1,0:T(8,128)(2,1)S(1)}, u32[]{:S(2)}, u32[]{:S(2)}) async-start(bf16[16,6,3584]{2,1,0:T(8,128)(2,1)} %convert_element_type.103), calls=%async_computation.2 | async-start | bytes 1835008 | tf_op jit(solution)/shard_map/all_to_all | solution.py:70
  111.1 20.6 %all-to-all-done.1 = bf16[16,6,3584]{2,1,0:T(8,128)(2,1)S(1)} async-done(((bf16[16,6,3584]{2,1,0:T(8,128)(2,1)}), bf16[16,6,3584]{2,1,0:T(8,128)(2,1)S(1)}, u32[]{:S(2)}, u32[]{:S(2)}) %all-to-all-start.1) | async-done | bytes 688160 | tf_op jit(solution)/shard_map/all_to_all | solution.py:70
  131.7 0.2 reshape.138
  132.0 0.5 multiply_reduce_fusion
  132.5 0.4 convolution_convert_fusion.2
  132.9 0.2 reshape.139
  133.1 28.3 %all_to_all.21 = bf16[16,6,3584]{2,1,0:T(8,128)(2,1)S(1)} all-to-all(bf16[16,6,3584]{2,1,0:T(8,128)(2,1)S(1)} %reshape.139), channel_id=1, replica_groups=mesh['dp'=2,'ep'=16] {'ep'}, dimensions={0} | all-to-all | bytes 1376256 | tf_op jit(solution)/shard_map/all_to_all | solution.py:54
  161.4 1.1 reshape.140
  162.6 24.0 %all-gather.5.cloned.1.call-done = bf16[192,3584]{1,0:T(8,128)(2,1)} async-done(((bf16[96,3584]{1,0:T(8,128)(2,1)}), bf16[192,3584]{1,0:T(8,128)(2,1)}) %all-gather.5.cloned.1.call-update) | async-done | bytes 1376272 | tf_op jit(solution)/shard_map/all_gather | solution.py:61
  186.6 3.4 %fusion.6 = f32[192,512]{1,0:T(8,128)S(1)} fusion(bf16[192,3584]{1,0:T(8,128)(2,1)} %all-gather.5.cloned.1.call-done, bf16[2,1,3584,512]{3,2,1,0:T(8,128)(2,1)} %param.9), kind=kOutput, calls=%fused_computation.12 | convolution fusion | flops 704643072 | bytes 5439488 | tf_op jit(solution)/shard_map/dot_general | solution.py:62
  190.0 5.9 %convolution_convert_fusion = bf16[192,3584]{1,0:T(8,128)(2,1)} fusion(bf16[2,1,512,3584]{3,2,1,0:T(8,128)(2,1)} %param.11, bf16[192,3584]{1,0:T(8,128)(2,1)S(1)} %copy-done.2, bf16[2,1,3584,512]{3,2,1,0:T(8,128)(2,1)} %param.10, f32[192,512]{1,0:T(8,128)S(1)} %fusion.6), kind=kOutput, calls=%fused_computation | convolution fusion | flops 1410564096 | bytes 10485760 | tf_op jit(solution)/shard_map/dot_general | solution.py:65
  196.0 24.1 %reduce-scatter.5.cloned.1.call-done = bf16[96,3584]{1,0:T(8,128)(2,1)} async-done(((bf16[192,3584]{1,0:T(8,128)(2,1)}), bf16[96,3584]{1,0:T(8,128)(2,1)}) %reduce-scatter.5.cloned.1.call-update) | async-done | bytes 688144 | tf_op jit(solution)/shard_map/reduce_scatter | solution.py:67
  220.1 2.1 convert_element_type.114
  222.3 5.6 %all-to-all-start.3 = ((bf16[16,6,3584]{2,1,0:T(8,128)(2,1)}), bf16[16,6,3584]{2,1,0:T(8,128)(2,1)S(1)}, u32[]{:S(2)}, u32[]{:S(2)}) async-start(bf16[16,6,3584]{2,1,0:T(8,128)(2,1)} %convert_element_type.114), calls=%async_computation.5 | async-start | bytes 1835008 | tf_op jit(solution)/shard_map/all_to_all | solution.py:70
  227.9 42.9 %psum.7 = s32[2,16]{1,0:T(2,128)} all-reduce(s32[2,16]{1,0:T(2,128)S(1)} %pad_add_fusion), channel_id=1, replica_groups=mesh['dp'=2,'ep'=16] {'dp','ep'}, use_global_device_ids=true, to_apply=%region_16.17 | all-reduce | flops 32 | bytes 256 | tf_op jit(solution)/shard_map/psum | solution.py:44
  270.9 0.2 reshape.141
  271.1 1.0 fusion.2
  (29 shorter events, 1.3 us)
Async XLA Ops:
  7.2 62.4 %all-gather.3.cloned.1.call-start = ((), (), s32[]{:S(2)}) async-start(), calls=%async_computation.6 | async-start | bytes 2064384 | tf_op jit(solution)/shard_map/all_gather | solution.py:61
  44.6 58.5 %reduce-scatter.3.cloned.1.call-start = ((), (), s32[]{:S(2)}) async-start(), calls=%async_computation.7 | async-start | bytes 2064384 | tf_op jit(solution)/shard_map/reduce_scatter | solution.py:67
  69.6 3.4 %copy-start.1 = (bf16[192,3584]{1,0:T(8,128)(2,1)S(1)}, bf16[192,3584]{1,0:T(8,128)(2,1)}, u32[]{:S(2)}) copy-start(bf16[192,3584]{1,0:T(8,128)(2,1)} %all-gather.3.cloned.1.call-done) | copy-start | bytes 4128772
  79.0 53.0 %copy-start = (bf16[8,3584]{1,0:T(8,128)(2,1)S(1)}, bf16[8,3584]{1,0:T(8,128)(2,1)}, u32[]{:S(2)}) copy-start(bf16[8,3584]{1,0:T(8,128)(2,1)} %param.6) | copy-start | bytes 172036
  105.3 26.4 %all-to-all-start.1 = ((bf16[16,6,3584]{2,1,0:T(8,128)(2,1)}), bf16[16,6,3584]{2,1,0:T(8,128)(2,1)S(1)}, u32[]{:S(2)}, u32[]{:S(2)}) async-start(bf16[16,6,3584]{2,1,0:T(8,128)(2,1)} %convert_element_type.103), calls=%async_computation.2 | async-start | bytes 1835008 | tf_op jit(solution)/shard_map/all_to_all | solution.py:70
  110.9 75.7 %all-gather.5.cloned.1.call-start = ((), (), s32[]{:S(2)}) async-start(), calls=%async_computation.8 | async-start | bytes 2064384 | tf_op jit(solution)/shard_map/all_gather | solution.py:61
  162.5 57.6 %reduce-scatter.5.cloned.1.call-start = ((), (), s32[]{:S(2)}) async-start(), calls=%async_computation.9 | async-start | bytes 2064384 | tf_op jit(solution)/shard_map/reduce_scatter | solution.py:67
  186.6 3.4 %copy-start.2 = (bf16[192,3584]{1,0:T(8,128)(2,1)S(1)}, bf16[192,3584]{1,0:T(8,128)(2,1)}, u32[]{:S(2)}) copy-start(bf16[192,3584]{1,0:T(8,128)(2,1)} %all-gather.5.cloned.1.call-done) | copy-start | bytes 4128772
  222.3 48.6 %all-to-all-start.3 = ((bf16[16,6,3584]{2,1,0:T(8,128)(2,1)}), bf16[16,6,3584]{2,1,0:T(8,128)(2,1)S(1)}, u32[]{:S(2)}, u32[]{:S(2)}) async-start(bf16[16,6,3584]{2,1,0:T(8,128)(2,1)} %convert_element_type.114), calls=%async_computation.5 | async-start | bytes 1835008 | tf_op jit(solution)/shard_map/all_to_all | solution.py:70
Sparse Core Ops, SparseCore 0:
  44.7 24.8 all-gather.2
  79.1 23.9 reduce-scatter.2
  162.7 23.8 all-gather.4
  196.1 23.9 reduce-scatter.4
where the time goes:
time: 279 us
  waiting for transfers between devices  118 us (42%)
  blocking collectives  101 us (36%)
  matrix products  21.8 us (8%)
  between operations  13.9 us (5%)
  starting transfers between devices  11.4 us (4%)
  local copies, waits for them, and re-layouts  8.5 us (3%)
  other arithmetic  4.25 us (2%)
    all_to_all x2, blocking collectives, per_device(): lax.all_to_all(outgoing.reshape(n_ep, capacity, width), 'ep', split_axis=...  57.9 us
    all_gather x2, waiting for transfers between devices, per_device(): piece = lax.all_gather(arrived, 'dp', axis=0, tiled=True)  48.9 us
    reduce_scatter x2, waiting for transfers between devices, per_device(): lax.psum_scatter(parts.astype(jnp.float32).astype(jnp.bfloat16), 'dp', sc...  48.3 us
    psum x1, blocking collectives, per_device(): loads = lax.psum(table, ('dp', 'ep'))  42.9 us
    all_to_all x2, waiting for transfers between devices, per_device(): lax.all_to_all(summed.reshape(n_ep, capacity, width).astype(jnp.bfloat16)...  20.6 us
    dot_general x2, matrix products, per_device(): jnp.dot(hidden, weight_down, preferred_element_type=jnp.float32)  11.9 us
    all_to_all x2, starting transfers between devices, per_device(): lax.all_to_all(summed.reshape(n_ep, capacity, width).astype(jnp.bfloat16)...  11.2 us
    dot_general x2, matrix products, per_device(): gate = jnp.dot(piece, weight_gate, preferred_element_type=jnp.float32)  6.86 us
  transfers between devices with their start and end apart: 6, of which 5 were waited for; matrix products, arithmetic and copies ran while one was open for 0% of the time, Pallas kernels for 0%

commit v1 on v0

--- a/solution.py
+++ b/solution.py
@@ -1,6 +1,10 @@
+import functools
+
 import jax
 import jax.numpy as jnp
 from jax import lax
+from jax.experimental import pallas as pl
+from jax.experimental.pallas import tpu as pltpu
 from jax.sharding import PartitionSpec as P
 
 ROUTE_SCALE = 2.827
@@ -84,9 +88,368 @@
     return (state, loads)
 
 
+MESH = pl.DeviceIdType.MESH
+LANES = 128
+VMEM_BYTES = 60 * 1024 * 1024
+
+
+def moe_kernel(
+    n_z, x_ref, ids_ref, quant_ref, wg_hbm, wu_hbm, wd_hbm, out_ref, load_ref,
+    wg, wu, wd, mine, theirs, xown, xpar, state, hid, yown, ysend, r0, s1, r1, s2, r2, s3, r3,
+    sq_send, sq_recv, f_send, f_recv,
+    w_sem, first_sem, sq_sem, f_sem, ag_send, ag_recv, dd_send, dd_recv, y_send, y_recv,
+    s1_send, s1_recv, s2_send, s2_recv, s3_send, s3_recv,
+):
+    layers, tok, top = ids_ref.shape
+    width = x_ref.shape[1]
+    half = width // 2
+    ff = wg.shape[2]
+    chip = 2 * tok
+    dx = lax.axis_index("dp")
+    ep = lax.axis_index("ep")
+    c = ep % 2
+    b = (ep // 2) % 2
+    a = ep // 4
+    n_ep = 4 * n_z
+    own0 = pl.multiple_of(c * half, LANES)
+    par0 = pl.multiple_of((1 - c) * half, LANES)
+
+    def device(za, yb, xd, core):
+        return (xd, (za * 2 + yb) * 2 + core)
+
+    def block(za, yb, xd):
+        return (za * 2 + yb) * 2 + xd
+
+    def rows(blk):
+        return pl.ds(pl.multiple_of(blk * chip, chip), chip)
+
+    b1, x1 = (b + c) % 2, (dx + 1 - c) % 2
+    b2, x2 = (b + 1 - c) % 2, (dx + c) % 2
+    b3, x3 = 1 - b, 1 - dx
+    peer = device(a, b, dx, 1 - c)
+    p1 = device(a, b1, x1, c)
+    p2 = device(a, b2, x2, c)
+    order = [d for d in range(1, n_z)]
+    zs = [(a + d) % n_z for d in range(n_z)]
+
+    loads = []
+    for l in range(layers):
+        for i, (src, dst) in enumerate(((wg_hbm, wg), (wu_hbm, wu), (wd_hbm, wd))):
+            copy = pltpu.make_async_copy(src.at[l, 0], dst.at[l], w_sem.at[l, i])
+            copy.start()
+            loads.append(copy)
+
+    barrier = pltpu.get_barrier_semaphore()
+    targets = [peer, p1, p2] + [device(zs[d], b, dx, c) for d in order]
+    for target in targets:
+        pl.semaphore_signal(barrier, inc=1, device_id=target, device_id_type=MESH)
+
+    lane = lax.broadcasted_iota(jnp.int32, (tok, LANES), 1)
+    table = jnp.zeros((tok, LANES), jnp.float32)
+    for l in range(layers):
+        ids = ids_ref[l]
+        quant = quant_ref[l].astype(jnp.float32)
+        for k in range(top):
+            table += jnp.where(lane == ids[:, k : k + 1] + l * n_ep, quant[:, k : k + 1], 0.0)
+    mine[:, :width] = x_ref[...].astype(jnp.float32)
+    mine[:, width:] = table
+    pl.semaphore_wait(barrier, len(targets))
+
+    def remote(src, dst, send, recv, target):
+        return pltpu.make_async_remote_copy(
+            src_ref=src, dst_ref=dst, send_sem=send, recv_sem=recv, device_id=target, device_id_type=MESH
+        )
+
+    swap = remote(mine, theirs, first_sem.at[0], first_sem.at[1], peer)
+    swap.start()
+    swap.wait()
+
+    def by_core(own, other):
+        return jnp.concatenate(
+            [jnp.where(c == 0, own, other), jnp.where(c == 0, other, own)], axis=0
+        )
+
+    my_block = block(a, b, dx)
+    pairs = by_core(mine[:, width:], theirs[:, width:])
+    total = jnp.sum(mine[:, :width] * mine[:, :width], axis=1, keepdims=True)
+    total_other = jnp.sum(theirs[:, :width] * theirs[:, :width], axis=1, keepdims=True)
+    square = by_core(total, total_other)
+    state[...] = by_core(mine[:, pl.ds(own0, half)], theirs[:, pl.ds(own0, half)])
+
+    for l in range(layers):
+        if l > 0:
+            part = jnp.sum(state[...] * state[...], axis=1, keepdims=True)
+            sq_send[l] = jnp.broadcast_to(part, (chip, LANES))
+            swap = remote(sq_send.at[l], sq_recv.at[l], sq_sem.at[l, 0], sq_sem.at[l, 1], peer)
+            swap.start()
+            swap.wait()
+            square = (sq_send[l] + sq_recv[l])[:, :1]
+        normed = state[...] * lax.rsqrt(square / width + EPS)
+        xown[l, rows(my_block), :half] = normed.astype(jnp.bfloat16)
+        if l == 0:
+            xown[l, rows(my_block), half:] = pairs.astype(jnp.bfloat16)
+        cols = slice(0, half + LANES) if l == 0 else slice(0, half)
+        pending = []
+        slot = [0]
+
+        def forward(blk, target):
+            ref = xown.at[l, rows(blk), cols]
+            copy = remote(ref, ref, ag_send.at[l, slot[0]], ag_recv.at[l, blk], target)
+            copy.start()
+            slot[0] += 1
+            pending.append(copy)
+
+        def across(blk):
+            copy = remote(
+                xown.at[l, rows(blk), slice(0, half)], xpar.at[l, rows(blk)],
+                dd_send.at[l, blk], dd_recv.at[l, blk], peer,
+            )
+            copy.start()
+            pending.append(copy)
+
+        def arrived(blk):
+            ref = xown.at[l, rows(blk), cols]
+            remote(ref, ref, ag_send.at[l, 0], ag_recv.at[l, blk], p1).wait_recv()
+
+        for d in order:
+            forward(my_block, device(zs[d], b, dx, c))
+        forward(my_block, p1)
+        forward(my_block, p2)
+        across(my_block)
+        blk = block(a, b1, x1)
+        arrived(blk)
+        forward(blk, p2)
+        across(blk)
+        for d in order:
+            blk = block(zs[d], b, dx)
+            arrived(blk)
+            forward(blk, p1)
+            forward(blk, p2)
+            across(blk)
+        for d in order:
+            blk = block(zs[d], b1, x1)
+            arrived(blk)
+            forward(blk, p2)
+            across(blk)
+        for d in range(n_z):
+            for blk in (block(zs[d], b2, x2), block(zs[d], b3, x3)):
+                arrived(blk)
+                across(blk)
+        for blk in range(4 * n_z):
+            ref = xpar.at[l, rows(blk)]
+            remote(ref, ref, dd_send.at[l, blk], dd_recv.at[l, blk], peer).wait_recv()
+        for copy in pending:
+            copy.wait_send()
+        for copy in loads[3 * l : 3 * l + 3]:
+            copy.wait()
+
+        count = 4 * n_z * chip
+        score = xown[0, :, half:].astype(jnp.float32)
+        wide_lane = lax.broadcasted_iota(jnp.int32, (count, LANES), 1)
+        here = jnp.sum(jnp.where(wide_lane == l * n_ep + ep, score, 0.0), axis=1, keepdims=True)
+        every = jnp.sum(
+            jnp.where((wide_lane >= l * n_ep) & (wide_lane < (l + 1) * n_ep), score, 0.0),
+            axis=1, keepdims=True,
+        )
+        gate_row = ROUTE_SCALE * here / every
+        if l == 0:
+            seen = jnp.sum((score > 0.0).astype(jnp.float32), axis=0, keepdims=True).astype(jnp.int32)
+            for m in range(layers):
+                load_ref[m : m + 1, :] = seen[:, m * n_ep : (m + 1) * n_ep]
+
+        tile = 256
+
+        def expand(j, _):
+            col = pl.ds(pl.multiple_of(j * tile, tile), tile)
+
+            def product(weight):
+                return jnp.dot(
+                    xown[l, :, :half], weight[l, pl.ds(own0, half), col], preferred_element_type=jnp.float32
+                ) + jnp.dot(xpar[l], weight[l, pl.ds(par0, half), col], preferred_element_type=jnp.float32)
+
+            gate = product(wg)
+            upper = product(wu)
+            hid[:, col] = (jax.nn.silu(gate) * upper).astype(jnp.bfloat16)
+            return 0
+
+        lax.fori_loop(0, ff // tile, expand, 0)
+
+        def down(base, j):
+            return gate_row * jnp.dot(
+                hid[...], wd[l, :, pl.ds(pl.multiple_of(base + j * tile, LANES), tile)],
+                preferred_element_type=jnp.float32,
+            )
+
+        def crossing(j):
+            col = pl.ds(pl.multiple_of(j * tile, tile), tile)
+            return remote(ysend.at[l, :, col], r0.at[l, :, col], y_send.at[l, j], y_recv.at[l, j], peer)
+
+        def down_par(j, _):
+            ysend[l, :, pl.ds(pl.multiple_of(j * tile, tile), tile)] = down(par0, j).astype(jnp.bfloat16)
+            crossing(j).start()
+            return 0
+
+        def down_own(j, _):
+            yown[:, pl.ds(pl.multiple_of(j * tile, tile), tile)] = down(own0, j)
+            return 0
+
+        lax.fori_loop(0, half // tile, down_par, 0)
+        lax.fori_loop(0, half // tile, down_own, 0)
+        for j in range(half // tile):
+            crossing(j).wait()
+
+        def local(blk):
+            return yown[rows(blk), :] + r0[l, rows(blk), :].astype(jnp.float32)
+
+        def part_of(k):
+            return pl.ds(k * chip, chip)
+
+        turn = order + [0]
+        sends = []
+        for d in turn:
+            for q, (yb, xd) in enumerate(((b3, x3), (b2, x2))):
+                k = 2 * d + q
+                s1[l, part_of(k), :] = local(block(zs[d], yb, xd)).astype(jnp.bfloat16)
+                copy = remote(
+                    s1.at[l, part_of(k)], r1.at[l, part_of(k)], s1_send.at[l, k], s1_recv.at[l, k], p2
+                )
+                copy.start()
+                sends.append(copy)
+
+        def got(buf, k, send, recv):
+            ref = buf.at[l, part_of(k)]
+            remote(ref, ref, send.at[l, k], recv.at[l, k], p1).wait_recv()
+            return buf[l, part_of(k), :].astype(jnp.float32)
+
+        def second(d):
+            s2[l, part_of(d), :] = (
+                local(block(zs[d], b1, x1)) + got(r1, 2 * d, s1_send, s1_recv)
+            ).astype(jnp.bfloat16)
+            copy = remote(s2.at[l, part_of(d)], r2.at[l, part_of(d)], s2_send.at[l, d], s2_recv.at[l, d], p1)
+            copy.start()
+            sends.append(copy)
+
+        def third(d):
+            value = (
+                local(block(zs[d], b, dx))
+                + got(r1, 2 * d + 1, s1_send, s1_recv)
+                + got(r2, d, s2_send, s2_recv)
+            )
+            if d == 0:
+                return value
+            s3[l, part_of(d), :] = value.astype(jnp.bfloat16)
+            copy = remote(
+                s3.at[l, part_of(d)], r3.at[l, part_of(d)], s3_send.at[l, d], s3_recv.at[l, d],
+                device(zs[d], b, dx, c),
+            )
+            copy.start()
+            sends.append(copy)
+            return None
+
+        for i, d in enumerate(turn):
+            second(d)
+            if i > 0:
+                third(turn[i - 1])
+        branch = third(0)
+        for d in order:
+            branch = branch + got(r3, d, s3_send, s3_recv)
+        state[...] = (state[...] + branch).astype(jnp.bfloat16).astype(jnp.float32)
+        for copy in sends:
+            copy.wait_send()
+
+    low, high = state[:tok, :], state[tok:, :]
+    f_send[...] = jnp.where(c == 0, high, low)
+    swap = remote(f_send, f_recv, f_sem.at[0], f_sem.at[1], peer)
+    swap.start()
+    out_ref[:, pl.ds(own0, half)] = jnp.where(c == 0, low, high).astype(out_ref.dtype)
+    swap.wait()
+    out_ref[:, pl.ds(par0, half)] = f_recv[...].astype(out_ref.dtype)
+
+
+def scratch_list(n_z, layers, tok, width, ff):
+    half, chip = width // 2, 2 * tok
+    count = 4 * n_z * chip
+    blocks = 4 * n_z
+    bf16, f32 = jnp.bfloat16, jnp.float32
+    buffers = [
+        ((layers, width, ff), bf16),
+        ((layers, width, ff), bf16),
+        ((layers, ff, width), bf16),
+        ((tok, width + LANES), f32),
+        ((tok, width + LANES), f32),
+        ((layers, count, half + LANES), bf16),
+        ((layers, count, half), bf16),
+        ((chip, half), f32),
+        ((count, ff), bf16),
+        ((count, half), f32),
+        ((layers, count, half), bf16),
+        ((layers, count, half), bf16),
+        ((layers, count // 2, half), bf16),
+        ((layers, count // 2, half), bf16),
+        ((layers, count // 4, half), bf16),
+        ((layers, count // 4, half), bf16),
+        ((layers, count // 4, half), bf16),
+        ((layers, count // 4, half), bf16),
+        ((layers, chip, LANES), f32),
+        ((layers, chip, LANES), f32),
+        ((tok, half), f32),
+        ((tok, half), f32),
+    ]
+    sems = [
+        (layers, 3), (2,), (layers, 2), (2,),
+        (layers, blocks), (layers, blocks), (layers, blocks), (layers, blocks),
+        (layers, max(1, half // 256)), (layers, max(1, half // 256)),
+        (layers, 2 * n_z), (layers, 2 * n_z), (layers, n_z), (layers, n_z), (layers, n_z), (layers, n_z),
+    ]
+    size = 0
+    for shape, dtype in buffers:
+        bytes_of = jnp.dtype(dtype).itemsize
+        for dim in shape:
+            bytes_of *= dim
+        size += bytes_of
+    return buffers, sems, size
+
+
+def fused_device(n_z, tokens, expert_ids, quant_gates, w_gate, w_up, w_down):
+    layers, tok, _ = expert_ids.shape
+    width = tokens.shape[1]
+    ff = w_gate.shape[3]
+    buffers, sems, _ = scratch_list(n_z, layers, tok, width, ff)
+    vmem = pl.BlockSpec(memory_space=pltpu.VMEM)
+    hbm = pl.BlockSpec(memory_space=pl.ANY)
+    out, loads = pl.pallas_call(
+        functools.partial(moe_kernel, n_z),
+        out_shape=(
+            jax.ShapeDtypeStruct((tok, width), tokens.dtype),
+            jax.ShapeDtypeStruct((layers, 4 * n_z), jnp.int32),
+        ),
+        in_specs=[vmem, vmem, vmem, hbm, hbm, hbm],
+        out_specs=(vmem, vmem),
+        scratch_shapes=[pltpu.VMEM(shape, dtype) for shape, dtype in buffers]
+        + [pltpu.SemaphoreType.DMA(shape) for shape in sems],
+        compiler_params=pltpu.CompilerParams(
+            collective_id=0, has_side_effects=True, vmem_limit_bytes=VMEM_BYTES
+        ),
+    )(tokens, expert_ids, quant_gates, w_gate, w_up, w_down)
+    return (out, loads)
+
+
 def solution(mesh):
+    n_dp, n_ep = mesh.shape["dp"], mesh.shape["ep"]
+
+    def step(tokens, expert_ids, quant_gates, w_gate, w_up, w_down):
+        layers, tok, _ = expert_ids.shape
+        width, ff = tokens.shape[1], w_gate.shape[3]
+        fits = (
+            n_dp == 2 and n_ep % 4 == 0 and n_ep > 4 and tok == 8 and width % 512 == 0
+            and ff % 256 == 0 and layers * n_ep <= LANES
+        )
+        if fits and scratch_list(n_ep // 4, layers, tok, width, ff)[2] < VMEM_BYTES * 4 // 5:
+            return fused_device(n_ep // 4, tokens, expert_ids, quant_gates, w_gate, w_up, w_down)
+        return per_device(tokens, expert_ids, quant_gates, w_gate, w_up, w_down)
+
     return jax.shard_map(
-        per_device,
+        step,
         mesh=mesh,
         in_specs=(
             P(("dp", "ep"), None),

time: 279 us -> 88.7 us (0.32)
  waiting for transfers between devices: 118 us -> 0 us
  blocking collectives: 101 us -> 0 us
  Pallas kernels: 0 us -> 85.2 us
  matrix products: 21.8 us -> 0 us
  between operations: 13.9 us -> 0.64 us
  starting transfers between devices: 11.4 us -> 0 us
  local copies, waits for them, and re-layouts: 8.5 us -> 2.64 us
  other arithmetic: 4.25 us -> 0 us
    pallas_call x0 -> x1, Pallas kernels: none -> 85.2 us  [fused_device(): pl.pallas_call(functools.partial(moe_kernel, n_z), out_shape=(jax.ShapeDt...]
    all_to_all x2 -> x0, blocking collectives: 57.9 us -> none  [per_device(): lax.all_to_all(outgoing.reshape(n_ep, capacity, width), 'ep', split_axis=...]
    all_gather x2 -> x0, waiting for transfers between devices: 48.9 us -> none  [per_device(): piece = lax.all_gather(arrived, 'dp', axis=0, tiled=True)]
    reduce_scatter x2 -> x0, waiting for transfers between devices: 48.3 us -> none  [per_device(): lax.psum_scatter(parts.astype(jnp.float32).astype(jnp.bfloat16), 'dp', sc...]
    psum x1 -> x0, blocking collectives: 42.9 us -> none  [per_device(): loads = lax.psum(table, ('dp', 'ep'))]
    dot_general x8 -> x0, matrix products: 21.8 us -> none  [the longest x2 11.9 us: per_device(): jnp.dot(hidden, weight_down, preferred_element_type=jnp.float32)]
    all_to_all x2 -> x0, waiting for transfers between devices: 20.6 us -> none  [per_device(): lax.all_to_all(summed.reshape(n_ep, capacity, width).astype(jnp.bfloat16)...]
    all_to_all x2 -> x0, starting transfers between devices: 11.2 us -> none  [per_device(): lax.all_to_all(summed.reshape(n_ep, capacity, width).astype(jnp.bfloat16)...]
  transfers between devices with their start and end apart: 6 -> 0, of which waited for: 5 -> 0; matrix products, arithmetic and copies ran while one was open for 0% -> 0% of each run, Pallas kernels for 0% -> 0%
where the time goes in v1:
time: 88.7 us; the launch traced here: 88.4 us
  Pallas kernels  85.2 us (96%)
  local copies, waits for them, and re-layouts  2.64 us (3%)
    pallas_call x1, Pallas kernels, fused_device(): pl.pallas_call(functools.partial(moe_kernel, n_z), out_shape=(jax.ShapeDt...  85.2 us
    unnamed x2, local copies, waits for them, and re-layouts  2.64 us

profile of v1, /device:TPU:0, one launch (start us, length us, event | category | flops | bytes accessed | tf_op | source)
XLA Modules:
  0.0 88.4 jit_solution(3214104615541680392)
XLA Ops:
  0.6 85.2 %shard_map.77 = (bf16[8,3584]{1,0:T(8,128)(2,1)}, s32[2,16]{1,0:T(2,128)}) custom-call(bf16[8,3584]{1,0:T(8,128)(2,1)} %x_ref.1, s32[2,8,8]{2,1,0:T(8,128)} %ids_ref.1, s32[2,8,8]{2,1,0:T(8,128)} %quant_ref.1, bf16[2,1,3584,512]{3,2,1,0:T(8,128)(2,1)} %wg_hbm.1, bf16[2,1,3584,512]{3,2,1,0:T(8,128)(2,1)} %wu_hbm.1, bf16[2,1,512,3584]{3,2,1,0:T(8,128)(2,1)} %wd_hbm.1), custom_call_target="tpu_custom_call" | custom-call | tf_op jit(solution)/shard_map/pallas_call | solution.py:420
  85.8 1.4 %copy.10 = bf16[8,3584]{1,0:T(8,128)(2,1)} copy(bf16[8,3584]{1,0:T(8,128)(2,1)} %get-tuple-element.4) | data formatting | bytes 114688
  87.2 1.2 %copy.11 = s32[2,16]{1,0:T(2,128)} copy(s32[2,16]{1,0:T(2,128)} %get-tuple-element.5) | data formatting | bytes 256
